TPU v7x, 256 devices: a whole 4x4x8 slice. The times are simulated.
256 devices in a mesh: dp: 16 (over z, y_lo), mp: 16 (over y_hi, x, core).
Axes of the slice: x: 4, y: 4 (y_hi: 2, y_lo: 2; y = y_hi * 2 + y_lo), z: 8, core: 2. Of those that a mesh axis runs over, the one named last changes fastest.
Arguments:
- gradient: bfloat16 [1, 4096, 4096], P(None, 'mp', 'dp'), may hold values from -6 to 6
- first_moment: float32 [1, 4096, 4096], P(None, 'mp', 'dp'), may hold values from -3 to 3
- second_moment: float32 [1, 4096, 4096], P(None, 'mp', 'dp'), may hold values from 0.0625 to 1
- left_factor: float32 [1, 4096, 4096], P(None, 'mp', 'dp'), may hold values from -18 to 18
- right_factor: float32 [1, 4096, 4096], P(None, 'mp', 'dp'), may hold values from -18 to 18
- left_basis: bfloat16 [1, 4096, 4096], P(None, 'dp', 'mp'), may hold values from -0.09375 to 0.09375
- right_basis: bfloat16 [1, 4096, 4096], P(None, 'mp', 'dp'), may hold values from -0.09375 to 0.09375
Outputs:
- new_first_moment: float32 [1, 4096, 4096], P(None, 'mp', 'dp')
- new_second_moment: float32 [1, 4096, 4096], P(None, 'mp', 'dp')
- new_left_factor: float32 [1, 4096, 4096], P(None, 'mp', 'dp')
- new_right_factor: float32 [1, 4096, 4096], P(None, 'mp', 'dp')
- update: bfloat16 [1, 4096, 4096], P(None, 'mp', 'dp')
All inputs are finite; a program needn't handle non-finite values.
Results may differ from a plain program's by a relative error of at most 0.014.
Values may be sent and summed in bfloat16 or wider, within the bound.
No kernel may reach another device: no remote copies, remote signals or barrier semaphores. Data moves between devices by JAX's collectives and lax.ppermute only.
A program may use at most 64 MiB of HBM per device.

v0:
```python
import jax
import jax.numpy as jnp
from jax import lax
from jax.sharding import PartitionSpec as P

decay_moment = 0.95
decay_factor = 0.95
epsilon = 1e-08


def in_one_piece(arrays, axis, dim, along):
    widths = [a.shape[along] for a in arrays]
    both = jnp.concatenate(arrays, axis=along)
    whole = lax.all_gather(both, axis, axis=dim, tiled=True)
    return tuple(jnp.split(whole, [sum(widths[:k]) for k in range(1, len(widths))], axis=along))


def turned_gather(arrays, axis, dims):
    turned = [jnp.moveaxis(a, dim, 0) for a, dim in zip(arrays, dims)]
    both = jnp.concatenate([t.reshape(len(t), -1) for t in turned], axis=1)
    whole, at, gathered = (lax.all_gather(both, axis, axis=0, tiled=True), 0, [])
    for t, dim in zip(turned, dims):
        section = whole[:, at : at + t[0].size].reshape(-1, *t.shape[1:])
        gathered.append(jnp.moveaxis(section, 0, dim))
        at += t[0].size
    return tuple(gathered)


def in_order(pieces, dim):
    lengths = list(pieces.shape[1:])
    lengths[dim] *= pieces.shape[0]
    return jnp.moveaxis(pieces, 0, dim).reshape(lengths)


def from_everyone(x, axis):
    length = lax.axis_size(axis)
    return lax.all_to_all(jnp.broadcast_to(x[None], (length, *x.shape)), axis, 0, 0, tiled=True)


def collect(x, axis, dim):
    return in_order(from_everyone(x, axis), dim)


def split_up(x, dim, length):
    lengths = x.shape
    pieces = x.reshape(*lengths[:dim], length, lengths[dim] // length, *lengths[dim + 1 :])
    return jnp.moveaxis(pieces, dim, 0)


def summed_on_arrival(x, axis, dim):
    pieces = split_up(x, dim, lax.axis_size(axis))
    arrived = lax.all_to_all(pieces, axis, split_axis=0, concat_axis=0, tiled=True)
    return arrived.astype(jnp.float32).sum(axis=0)


def per_device(
    gradient, first_moment, second_moment, left_factor, right_factor, left_basis, right_basis
):
    scale = 1.0 - decay_factor
    column_grad, column_right = in_one_piece((gradient, right_basis), "mp", 1, 0)
    row_grad, column_left = turned_gather((gradient, left_basis), "dp", (2, 1))
    row_block = lax.all_to_all(column_grad, "dp", split_axis=1, concat_axis=2, tiled=True)
    column_block = lax.all_to_all(row_grad, "mp", split_axis=2, concat_axis=1, tiled=True)
    left_sum = jnp.einsum("brc,bkc->brk", row_grad, row_block, preferred_element_type=jnp.float32)
    right_sum = jnp.einsum(
        "bkr,bkc->brc", column_block, column_grad, preferred_element_type=jnp.float32
    )
    rotated_left = jnp.einsum(
        "bkr,bkc->brc", column_left, column_grad, preferred_element_type=jnp.float32
    ).astype(jnp.bfloat16)
    rotated = jnp.einsum(
        "brn,bnc->brc",
        collect(rotated_left, "dp", 2),
        column_right,
        preferred_element_type=jnp.float32,
    )
    new_first = decay_moment * first_moment + (1.0 - decay_moment) * rotated
    new_second = decay_moment * second_moment + (1.0 - decay_moment) * rotated * rotated
    direction = (new_first / (jnp.sqrt(new_second) + epsilon)).astype(jnp.bfloat16)
    back_term = jnp.einsum(
        "bkr,brc->bkc", column_left, direction, preferred_element_type=jnp.float32
    )
    back_sum = summed_on_arrival(back_term.astype(jnp.bfloat16), "mp", 1)
    back_rows = back_sum.astype(jnp.bfloat16)
    update_term = jnp.einsum(
        "brc,bkc->brk", back_rows, column_right, preferred_element_type=jnp.float32
    )
    update_sum = summed_on_arrival(update_term.astype(jnp.bfloat16), "dp", 2)
    new_left = decay_factor * left_factor + scale * left_sum
    new_right = decay_factor * right_factor + scale * right_sum
    return (new_first, new_second, new_left, new_right, update_sum.astype(jnp.bfloat16))


def solution(mesh):
    in_specs = (
        P(None, "mp", "dp"),
        P(None, "mp", "dp"),
        P(None, "mp", "dp"),
        P(None, "mp", "dp"),
        P(None, "mp", "dp"),
        P(None, "dp", "mp"),
        P(None, "mp", "dp"),
    )
    out_specs = (
        P(None, "mp", "dp"),
        P(None, "mp", "dp"),
        P(None, "mp", "dp"),
        P(None, "mp", "dp"),
        P(None, "mp", "dp"),
    )
    return jax.shard_map(
        per_device, mesh=mesh, in_specs=in_specs, out_specs=out_specs, check_vma=False
    )
```

profile of v0, /device:TPU:16, one launch (start us, length us, event | category | flops | bytes accessed | tf_op | source)
XLA Modules:
  0.0 455.4 jit_solution(4310972106720529222)
XLA Ops:
  11.6 100.3 %all-gather.3.cloned.1.call-done = bf16[4096,512]{1,0:T(8,128)(2,1)} async-done(((bf16[256,512]{1,0:T(8,128)(2,1)}), bf16[4096,512]{1,0:T(8,128)(2,1)}) %all-gather.3.cloned.1.call-update) | async-done | bytes 4194320 | tf_op jit(solution)/shard_map/all_gather | solution.py:21
  112.0 62.4 %all-gather.5.cloned.1.call-done = bf16[2,4096,256]{2,1,0:T(8,128)(2,1)} async-done(((bf16[2,256,256]{2,1,0:T(8,128)(2,1)}), bf16[2,4096,256]{2,1,0:T(8,128)(2,1)}) %all-gather.5.cloned.1.call-update) | async-done | bytes 4194320 | tf_op jit(solution)/shard_map/all_gather | solution.py:14
  174.4 3.0 fusion.28
  179.0 8.7 %all-to-all-start = ((bf16[16,1,256,256]{2,3,1,0:T(8,128)(2,1)}), bf16[16,1,256,256]{2,3,1,0:T(8,128)(2,1)}, u32[]{:S(2)}, u32[]{:S(2)}) async-start(bf16[16,1,256,256]{2,3,1,0:T(8,128)(2,1)} %broadcast_in_dim.2), calls=%async_computation | async-start | bytes 4194304 | tf_op jit(solution)/shard_map/all_to_all | solution.py:37
  189.4 25.0 %copy.45 = bf16[1,256,4096]{1,0,2:T(2,128)(2,1)} copy(bf16[1,256,4096]{1,2,0:T(8,128)(2,1)S(1)} %slice_bitcast_fusion.3) | data formatting | bytes 4194304 | tf_op jit(solution)/shard_map/transpose | solution.py:24
  215.0 21.6 %reduce.5 = bf16[4096,256]{1,0:T(8,128)(2,1)S(1)} reduce(bf16[4096,1,256]{2,1,0:T(2,128)(2,1)} %bitcast.92, bf16[]{:T(256)} %broadcast.21), dimensions={1}, to_apply=%bitcast.90.reduce_sub_computation | reduce | bytes 4194306
  238.7 6.8 %all-to-all-start.2 = ((bf16[16,2,32768]{2,1,0:T(2,128)(2,1)}), bf16[16,2,32768]{2,1,0:T(2,128)(2,1)S(1)}, u32[]{:S(2)}, u32[]{:S(2)}) async-start(bf16[16,2,32768]{2,1,0:T(2,128)(2,1)} %reshape.85), calls=%async_computation.2 | async-start | bytes 4194304 | tf_op jit(solution)/shard_map/all_to_all | solution.py:63
  245.5 3.1 fusion.35
  251.0 21.6 %all-to-all-done.2 = bf16[16,2,32768]{2,1,0:T(2,128)(2,1)S(1)} async-done(((bf16[16,2,32768]{2,1,0:T(2,128)(2,1)}), bf16[16,2,32768]{2,1,0:T(2,128)(2,1)S(1)}, u32[]{:S(2)}, u32[]{:S(2)}) %all-to-all-start.2) | async-done | bytes 2097184 | tf_op jit(solution)/shard_map/all_to_all | solution.py:63
  272.6 6.6 %all-to-all-start.3 = ((bf16[16,1,256,256]{3,2,1,0:T(8,128)(2,1)}), bf16[16,1,256,256]{3,2,1,0:T(8,128)(2,1)}, u32[]{:S(2)}, u32[]{:S(2)}) async-start(bf16[16,1,256,256]{3,2,1,0:T(8,128)(2,1)} %bitcast.101), calls=%async_computation.3 | async-start | bytes 4194304 | tf_op jit(solution)/shard_map/all_to_all | solution.py:52
  280.8 25.0 %copy.46 = bf16[1,4096,256]{2,0,1:T(2,128)(2,1)} copy(bf16[1,4096,256]{2,1,0:T(8,128)(2,1)S(1)} %slice-done) | data formatting | bytes 4194304 | tf_op jit(solution)/shard_map/split | solution.py:15
  305.8 22.9 %reduce.4 = bf16[4096,256]{1,0:T(8,128)(2,1)} reduce(bf16[4096,1,256]{2,1,0:T(2,128)(2,1)} %bitcast.93, bf16[]{:T(256)} %broadcast.21), dimensions={1}, to_apply=%bitcast.91.reduce_sub_computation | reduce | bytes 4194306
  328.8 4.0 reshape.83
  332.7 8.1 %all-to-all-start.1 = ((bf16[16,2,32768]{2,1,0:T(2,128)(2,1)}), bf16[16,2,32768]{2,1,0:T(2,128)(2,1)}, u32[]{:S(2)}, u32[]{:S(2)}) async-start(bf16[16,2,32768]{2,1,0:T(2,128)(2,1)} %reshape.83), calls=%async_computation.1 | async-start | bytes 4194304 | tf_op jit(solution)/shard_map/all_to_all | solution.py:62
  347.8 43.6 %all-to-all-done.1 = bf16[16,2,32768]{2,1,0:T(2,128)(2,1)} async-done(((bf16[16,2,32768]{2,1,0:T(2,128)(2,1)}), bf16[16,2,32768]{2,1,0:T(2,128)(2,1)}, u32[]{:S(2)}, u32[]{:S(2)}) %all-to-all-start.1) | async-done | bytes 2097184 | tf_op jit(solution)/shard_map/all_to_all | solution.py:62
  391.4 4.7 %all-to-all-start.4 = ((bf16[16,1,256,256]{3,2,1,0:T(8,128)(2,1)}), bf16[16,1,256,256]{3,2,1,0:T(8,128)(2,1)}, u32[]{:S(2)}, u32[]{:S(2)}) async-start(bf16[16,1,256,256]{3,2,1,0:T(8,128)(2,1)} %bitcast.98), calls=%async_computation.4 | async-start | bytes 4194304 | tf_op jit(solution)/shard_map/all_to_all | solution.py:52
  396.1 6.8 %reshape.86 = bf16[4096,1,256]{2,1,0:T(2,128)(2,1)} reshape(bf16[16,2,32768]{2,1,0:T(2,128)(2,1)S(1)} %all-to-all-done.2) | data formatting | bytes 4194304
  402.9 2.5 copy.39
  408.0 3.7 fusion.25
  411.6 10.5 %reshape.84 = bf16[4096,1,256]{2,1,0:T(2,128)(2,1)} reshape(bf16[16,2,32768]{2,1,0:T(2,128)(2,1)} %all-to-all-done.1) | data formatting | bytes 4194304
  422.1 2.5 copy.38
  427.1 3.7 fusion.22
  430.8 15.2 %all-to-all-done.4 = bf16[16,1,256,256]{3,2,1,0:T(8,128)(2,1)} async-done(((bf16[16,1,256,256]{3,2,1,0:T(8,128)(2,1)}), bf16[16,1,256,256]{3,2,1,0:T(8,128)(2,1)}, u32[]{:S(2)}, u32[]{:S(2)}) %all-to-all-start.4) | async-done | bytes 2097184 | tf_op jit(solution)/shard_map/all_to_all | solution.py:52
  445.9 2.6 reduce_sum.27
  (37 shorter events, 26.2 us)
Async XLA Ops:
  7.2 104.8 %all-gather.3.cloned.1.call-start = ((), (), s32[]{:S(2)}) async-start(), calls=%async_computation.5 | async-start | bytes 4456448 | tf_op jit(solution)/shard_map/all_gather | solution.py:21
  9.9 164.5 %all-gather.5.cloned.1.call-start = ((), (), s32[]{:S(2)}) async-start(), calls=%async_computation.6 | async-start | bytes 4456448 | tf_op jit(solution)/shard_map/all_gather | solution.py:14
  179.0 59.7 %all-to-all-start = ((bf16[16,1,256,256]{2,3,1,0:T(8,128)(2,1)}), bf16[16,1,256,256]{2,3,1,0:T(8,128)(2,1)}, u32[]{:S(2)}, u32[]{:S(2)}) async-start(bf16[16,1,256,256]{2,3,1,0:T(8,128)(2,1)} %broadcast_in_dim.2), calls=%async_computation | async-start | bytes 4194304 | tf_op jit(solution)/shard_map/all_to_all | solution.py:37
  238.7 6.8 %copy-start.1 = (f32[1,256,256]{2,1,0:T(8,128)S(1)}, f32[1,256,256]{2,1,0:T(8,128)}, u32[]{:S(2)}) copy-start(f32[1,256,256]{2,1,0:T(8,128)} %param.9) | copy-start | bytes 786436
  238.7 6.8 %copy-start.2 = (f32[1,256,256]{2,1,0:T(8,128)S(1)}, f32[1,256,256]{2,1,0:T(8,128)}, u32[]{:S(2)}) copy-start(f32[1,256,256]{2,1,0:T(8,128)} %param.8) | copy-start | bytes 786436
  238.7 33.9 %all-to-all-start.2 = ((bf16[16,2,32768]{2,1,0:T(2,128)(2,1)}), bf16[16,2,32768]{2,1,0:T(2,128)(2,1)S(1)}, u32[]{:S(2)}, u32[]{:S(2)}) async-start(bf16[16,2,32768]{2,1,0:T(2,128)(2,1)} %reshape.85), calls=%async_computation.2 | async-start | bytes 4194304 | tf_op jit(solution)/shard_map/all_to_all | solution.py:63
  245.5 3.5 copy-start
  248.6 2.4 copy-start.5
  248.6 2.4 copy-start.6
  272.6 60.1 %all-to-all-start.3 = ((bf16[16,1,256,256]{3,2,1,0:T(8,128)(2,1)}), bf16[16,1,256,256]{3,2,1,0:T(8,128)(2,1)}, u32[]{:S(2)}, u32[]{:S(2)}) async-start(bf16[16,1,256,256]{3,2,1,0:T(8,128)(2,1)} %bitcast.101), calls=%async_computation.3 | async-start | bytes 4194304 | tf_op jit(solution)/shard_map/all_to_all | solution.py:52
  279.2 1.6 slice-start
  332.7 58.7 %all-to-all-start.1 = ((bf16[16,2,32768]{2,1,0:T(2,128)(2,1)}), bf16[16,2,32768]{2,1,0:T(2,128)(2,1)}, u32[]{:S(2)}, u32[]{:S(2)}) async-start(bf16[16,2,32768]{2,1,0:T(2,128)(2,1)} %reshape.83), calls=%async_computation.1 | async-start | bytes 4194304 | tf_op jit(solution)/shard_map/all_to_all | solution.py:62
  391.4 54.5 %all-to-all-start.4 = ((bf16[16,1,256,256]{3,2,1,0:T(8,128)(2,1)}), bf16[16,1,256,256]{3,2,1,0:T(8,128)(2,1)}, u32[]{:S(2)}, u32[]{:S(2)}) async-start(bf16[16,1,256,256]{3,2,1,0:T(8,128)(2,1)} %bitcast.98), calls=%async_computation.4 | async-start | bytes 4194304 | tf_op jit(solution)/shard_map/all_to_all | solution.py:52
  405.5 2.5 copy-start.3
  424.7 2.4 copy-start.4
Sparse Core Ops, SparseCore 0:
  10.3 101.6 all-gather.2
  115.3 59.0 all-gather.4
where the time goes:
time: 456 us; the launch traced here: 455 us
  waiting for transfers between devices  243 us (53%)
  local copies, waits for them, and re-layouts  92.9 us (20%)
  other arithmetic  52.3 us (11%)
  starting transfers between devices  35 us (8%)
  matrix products  17.8 us (4%)
  between operations  14.2 us (3%)
    all_gather x1, waiting for transfers between devices, turned_gather(): lax.all_gather(both, axis, axis=0, tiled=True)  100 us
    all_gather x1, waiting for transfers between devices, in_one_piece(): whole = lax.all_gather(both, axis, axis=dim, tiled=True)  62.4 us
    unnamed x2, other arithmetic  44.5 us
    all_to_all x1, waiting for transfers between devices, per_device(): lax.all_to_all(column_grad, 'dp', split_axis=1, concat_axis=2, tiled=True)  43.6 us
    unnamed x23, local copies, waits for them, and re-layouts  31 us
    transpose x2, local copies, waits for them, and re-layouts, turned_gather(): gathered.append(jnp.moveaxis(section, 0, dim))  26.8 us
    split x3, local copies, waits for them, and re-layouts, in_one_piece(): jnp.split(whole, [sum(widths[:k]) for k in range(1, len(widths))], axis=a...  26.6 us
    all_to_all x1, waiting for transfers between devices, per_device(): lax.all_to_all(row_grad, 'mp', split_axis=2, concat_axis=1, tiled=True)  21.6 us
  transfers between devices with their start and end apart: 7, of which 5 were waited for; matrix products, arithmetic and copies ran while one was open for 33% of the time, Pallas kernels for 0%

commit v1 on v0

--- a/solution.py
+++ b/solution.py
@@ -18,7 +18,13 @@
 def turned_gather(arrays, axis, dims):
     turned = [jnp.moveaxis(a, dim, 0) for a, dim in zip(arrays, dims)]
     both = jnp.concatenate([t.reshape(len(t), -1) for t in turned], axis=1)
-    whole, at, gathered = (lax.all_gather(both, axis, axis=0, tiled=True), 0, [])
+    whole, at, gathered = (
+        jnp.concatenate(
+            lax.all_to_all(jnp.stack([both] * lax.axis_size(axis)), axis, 0, 0), axis=0
+        ),
+        0,
+        [],
+    )
     for t, dim in zip(turned, dims):
         section = whole[:, at : at + t[0].size].reshape(-1, *t.shape[1:])
         gathered.append(jnp.moveaxis(section, 0, dim))

time: 456 us -> 399 us (0.88)
  waiting for transfers between devices: 243 us -> 177 us
  starting transfers between devices: 35 us -> 41.2 us
    all_gather x1 -> x0, waiting for transfers between devices: 100 us -> none  [turned_gather(): lax.all_gather(both, axis, axis=0, tiled=True)]
    all_to_all x0 -> x1, waiting for transfers between devices: none -> 46.1 us  [turned_gather(): lax.all_to_all(jnp.stack([both] * lax.axis_size(axis)), axis, 0, 0)]
    all_gather x1, waiting for transfers between devices: 62.4 us -> 51.3 us  [in_one_piece(): whole = lax.all_gather(both, axis, axis=dim, tiled=True)]
    all_to_all x0 -> x1, starting transfers between devices: none -> 9.34 us  [turned_gather(): lax.all_to_all(jnp.stack([both] * lax.axis_size(axis)), axis, 0, 0)]
    unnamed x23 -> x21, local copies, waits for them, and re-layouts: 31 us -> 30.7 us
  transfers between devices with their start and end apart: 7 -> 7, of which waited for: 5 -> 5; matrix products, arithmetic and copies ran while one was open for 33% -> 39% of each run, Pallas kernels for 0% -> 0%
where the time goes in v1:
time: 399 us; the launch traced here: 398 us
  waiting for transfers between devices  177 us (44%)
  local copies, waits for them, and re-layouts  94.9 us (24%)
  other arithmetic  51.6 us (13%)
  starting transfers between devices  41.2 us (10%)
  matrix products  19.4 us (5%)
  between operations  14.2 us (4%)
    all_gather x1, waiting for transfers between devices, in_one_piece(): whole = lax.all_gather(both, axis, axis=dim, tiled=True)  51.3 us
    all_to_all x1, waiting for transfers between devices, turned_gather(): lax.all_to_all(jnp.stack([both] * lax.axis_size(axis)), axis, 0, 0)  46.1 us
    unnamed x2, other arithmetic  44.5 us
    all_to_all x1, waiting for transfers between devices, per_device(): lax.all_to_all(column_grad, 'dp', split_axis=1, concat_axis=2, tiled=True)  43.6 us
    unnamed x21, local copies, waits for them, and re-layouts  30.7 us
    transpose x2, local copies, waits for them, and re-layouts, turned_gather(): gathered.append(jnp.moveaxis(section, 0, dim))  26.8 us
    split x3, local copies, waits for them, and re-layouts, in_one_piece(): jnp.split(whole, [sum(widths[:k]) for k in range(1, len(widths))], axis=a...  26.6 us
    all_to_all x1, waiting for transfers between devices, per_device(): lax.all_to_all(row_grad, 'mp', split_axis=2, concat_axis=1, tiled=True)  20.3 us
  transfers between devices with their start and end apart: 7, of which 5 were waited for; matrix products, arithmetic and copies ran while one was open for 39% of the time, Pallas kernels for 0%

profile of v1, /device:TPU:16, one launch (start us, length us, event | category | flops | bytes accessed | tf_op | source)
XLA Modules:
  0.0 397.9 jit_solution(11445842321485780609)
XLA Ops:
  13.2 9.3 %all-to-all-start = ((bf16[16,256,512]{2,1,0:T(8,128)(2,1)}), bf16[16,256,512]{2,1,0:T(8,128)(2,1)}, u32[]{:S(2)}, u32[]{:S(2)}) async-start(bf16[16,256,512]{2,1,0:T(8,128)(2,1)} %stack.2), calls=%async_computation | async-start | bytes 8388608 | tf_op jit(solution)/shard_map/all_to_all | solution.py:23
  22.6 51.3 %all-gather.2.cloned.1.call-done = bf16[2,4096,256]{2,1,0:T(8,128)(2,1)} async-done(((bf16[2,256,256]{2,1,0:T(8,128)(2,1)}), bf16[2,4096,256]{2,1,0:T(8,128)(2,1)}) %all-gather.2.cloned.1.call-update) | async-done | bytes 4194320 | tf_op jit(solution)/shard_map/all_gather | solution.py:14
  73.9 46.1 %all-to-all-done = bf16[16,256,512]{2,1,0:T(8,128)(2,1)} async-done(((bf16[16,256,512]{2,1,0:T(8,128)(2,1)}), bf16[16,256,512]{2,1,0:T(8,128)(2,1)}, u32[]{:S(2)}, u32[]{:S(2)}) %all-to-all-start) | async-done | bytes 4194336 | tf_op jit(solution)/shard_map/all_to_all | solution.py:23
  120.0 3.0 fusion.28
  124.6 5.0 %all-to-all-start.1 = ((bf16[16,1,256,256]{2,3,1,0:T(8,128)(2,1)}), bf16[16,1,256,256]{2,3,1,0:T(8,128)(2,1)}, u32[]{:S(2)}, u32[]{:S(2)}) async-start(bf16[16,1,256,256]{2,3,1,0:T(8,128)(2,1)} %broadcast_in_dim.2), calls=%async_computation.1 | async-start | bytes 4194304 | tf_op jit(solution)/shard_map/all_to_all | solution.py:43
  131.4 25.0 %copy.45 = bf16[1,256,4096]{1,0,2:T(2,128)(2,1)} copy(bf16[1,256,4096]{1,2,0:T(8,128)(2,1)S(1)} %slice_bitcast_fusion.3) | data formatting | bytes 4194304 | tf_op jit(solution)/shard_map/transpose | solution.py:30
  156.9 21.6 %reduce.5 = bf16[4096,256]{1,0:T(8,128)(2,1)S(1)} reduce(bf16[4096,1,256]{2,1,0:T(2,128)(2,1)} %bitcast.93, bf16[]{:T(256)} %broadcast.23), dimensions={1}, to_apply=%bitcast.91.reduce_sub_computation | reduce | bytes 4194306
  180.6 7.4 %all-to-all-start.3 = ((bf16[16,2,32768]{2,1,0:T(2,128)(2,1)}), bf16[16,2,32768]{2,1,0:T(2,128)(2,1)S(1)}, u32[]{:S(2)}, u32[]{:S(2)}) async-start(bf16[16,2,32768]{2,1,0:T(2,128)(2,1)} %reshape.91), calls=%async_computation.3 | async-start | bytes 4194304 | tf_op jit(solution)/shard_map/all_to_all | solution.py:69
  188.1 3.0 fusion.35
  191.1 3.8 convolution_convert_fusion.1
  194.9 20.3 %all-to-all-done.3 = bf16[16,2,32768]{2,1,0:T(2,128)(2,1)S(1)} async-done(((bf16[16,2,32768]{2,1,0:T(2,128)(2,1)}), bf16[16,2,32768]{2,1,0:T(2,128)(2,1)S(1)}, u32[]{:S(2)}, u32[]{:S(2)}) %all-to-all-start.3) | async-done | bytes 2097184 | tf_op jit(solution)/shard_map/all_to_all | solution.py:69
  215.2 6.6 %all-to-all-start.4 = ((bf16[16,1,256,256]{3,2,1,0:T(8,128)(2,1)}), bf16[16,1,256,256]{3,2,1,0:T(8,128)(2,1)}, u32[]{:S(2)}, u32[]{:S(2)}) async-start(bf16[16,1,256,256]{3,2,1,0:T(8,128)(2,1)} %bitcast.102), calls=%async_computation.4 | async-start | bytes 4194304 | tf_op jit(solution)/shard_map/all_to_all | solution.py:58
  223.4 25.0 %copy.46 = bf16[1,4096,256]{2,0,1:T(2,128)(2,1)} copy(bf16[1,4096,256]{2,1,0:T(8,128)(2,1)S(1)} %slice-done) | data formatting | bytes 4194304 | tf_op jit(solution)/shard_map/split | solution.py:15
  248.4 22.9 %reduce.4 = bf16[4096,256]{1,0:T(8,128)(2,1)} reduce(bf16[4096,1,256]{2,1,0:T(2,128)(2,1)} %bitcast.94, bf16[]{:T(256)} %broadcast.23), dimensions={1}, to_apply=%bitcast.92.reduce_sub_computation | reduce | bytes 4194306
  271.3 4.0 %reshape.89 = bf16[16,2,32768]{2,1,0:T(2,128)(2,1)} reshape(bf16[4096,256]{1,0:T(8,128)(2,1)} %reduce.4) | data formatting | bytes 4194304
  275.3 8.1 %all-to-all-start.2 = ((bf16[16,2,32768]{2,1,0:T(2,128)(2,1)}), bf16[16,2,32768]{2,1,0:T(2,128)(2,1)}, u32[]{:S(2)}, u32[]{:S(2)}) async-start(bf16[16,2,32768]{2,1,0:T(2,128)(2,1)} %reshape.89), calls=%async_computation.2 | async-start | bytes 4194304 | tf_op jit(solution)/shard_map/all_to_all | solution.py:68
  290.4 43.6 %all-to-all-done.2 = bf16[16,2,32768]{2,1,0:T(2,128)(2,1)} async-done(((bf16[16,2,32768]{2,1,0:T(2,128)(2,1)}), bf16[16,2,32768]{2,1,0:T(2,128)(2,1)}, u32[]{:S(2)}, u32[]{:S(2)}) %all-to-all-start.2) | async-done | bytes 2097184 | tf_op jit(solution)/shard_map/all_to_all | solution.py:68
  334.0 4.7 %all-to-all-start.5 = ((bf16[16,1,256,256]{3,2,1,0:T(8,128)(2,1)}), bf16[16,1,256,256]{3,2,1,0:T(8,128)(2,1)}, u32[]{:S(2)}, u32[]{:S(2)}) async-start(bf16[16,1,256,256]{3,2,1,0:T(8,128)(2,1)} %bitcast.99), calls=%async_computation.5 | async-start | bytes 4194304 | tf_op jit(solution)/shard_map/all_to_all | solution.py:58
  338.7 6.8 %reshape.92 = bf16[4096,1,256]{2,1,0:T(2,128)(2,1)} reshape(bf16[16,2,32768]{2,1,0:T(2,128)(2,1)S(1)} %all-to-all-done.3) | data formatting | bytes 4194304
  350.5 3.7 fusion.25
  354.2 10.5 %reshape.90 = bf16[4096,1,256]{2,1,0:T(2,128)(2,1)} reshape(bf16[16,2,32768]{2,1,0:T(2,128)(2,1)} %all-to-all-done.2) | data formatting | bytes 4194304
  369.6 3.7 fusion.22
  373.3 15.2 %all-to-all-done.5 = bf16[16,1,256,256]{3,2,1,0:T(8,128)(2,1)} async-done(((bf16[16,1,256,256]{3,2,1,0:T(8,128)(2,1)}), bf16[16,1,256,256]{3,2,1,0:T(8,128)(2,1)}, u32[]{:S(2)}, u32[]{:S(2)}) %all-to-all-start.5) | async-done | bytes 2097184 | tf_op jit(solution)/shard_map/all_to_all | solution.py:58
  388.5 2.6 reduce_sum.27
  (35 shorter events, 30.5 us)
Async XLA Ops:
  7.2 66.8 %all-gather.2.cloned.1.call-start = ((), (), s32[]{:S(2)}) async-start(), calls=%async_computation.6 | async-start | bytes 4456448 | tf_op jit(solution)/shard_map/all_gather | solution.py:14
  13.2 106.8 %all-to-all-start = ((bf16[16,256,512]{2,1,0:T(8,128)(2,1)}), bf16[16,256,512]{2,1,0:T(8,128)(2,1)}, u32[]{:S(2)}, u32[]{:S(2)}) async-start(bf16[16,256,512]{2,1,0:T(8,128)(2,1)} %stack.2), calls=%async_computation | async-start | bytes 8388608 | tf_op jit(solution)/shard_map/all_to_all | solution.py:23
  124.6 56.0 %all-to-all-start.1 = ((bf16[16,1,256,256]{2,3,1,0:T(8,128)(2,1)}), bf16[16,1,256,256]{2,3,1,0:T(8,128)(2,1)}, u32[]{:S(2)}, u32[]{:S(2)}) async-start(bf16[16,1,256,256]{2,3,1,0:T(8,128)(2,1)} %broadcast_in_dim.2), calls=%async_computation.1 | async-start | bytes 4194304 | tf_op jit(solution)/shard_map/all_to_all | solution.py:43
  180.6 7.4 %copy-start = (f32[1,256,256]{2,1,0:T(8,128)S(1)}, f32[1,256,256]{2,1,0:T(8,128)}, u32[]{:S(2)}) copy-start(f32[1,256,256]{2,1,0:T(8,128)} %param.9) | copy-start | bytes 786436
  180.6 7.4 %copy-start.1 = (f32[1,256,256]{2,1,0:T(8,128)S(1)}, f32[1,256,256]{2,1,0:T(8,128)}, u32[]{:S(2)}) copy-start(f32[1,256,256]{2,1,0:T(8,128)} %param.8) | copy-start | bytes 786436
  180.6 34.5 %all-to-all-start.3 = ((bf16[16,2,32768]{2,1,0:T(2,128)(2,1)}), bf16[16,2,32768]{2,1,0:T(2,128)(2,1)S(1)}, u32[]{:S(2)}, u32[]{:S(2)}) async-start(bf16[16,2,32768]{2,1,0:T(2,128)(2,1)} %reshape.91), calls=%async_computation.3 | async-start | bytes 4194304 | tf_op jit(solution)/shard_map/all_to_all | solution.py:69
  191.0 3.9 copy-start.4
  191.0 3.9 copy-start.5
  215.2 60.1 %all-to-all-start.4 = ((bf16[16,1,256,256]{3,2,1,0:T(8,128)(2,1)}), bf16[16,1,256,256]{3,2,1,0:T(8,128)(2,1)}, u32[]{:S(2)}, u32[]{:S(2)}) async-start(bf16[16,1,256,256]{3,2,1,0:T(8,128)(2,1)} %bitcast.102), calls=%async_computation.4 | async-start | bytes 4194304 | tf_op jit(solution)/shard_map/all_to_all | solution.py:58
  221.8 1.6 slice-start
  275.3 58.7 %all-to-all-start.2 = ((bf16[16,2,32768]{2,1,0:T(2,128)(2,1)}), bf16[16,2,32768]{2,1,0:T(2,128)(2,1)}, u32[]{:S(2)}, u32[]{:S(2)}) async-start(bf16[16,2,32768]{2,1,0:T(2,128)(2,1)} %reshape.89), calls=%async_computation.2 | async-start | bytes 4194304 | tf_op jit(solution)/shard_map/all_to_all | solution.py:68
  334.0 54.5 %all-to-all-start.5 = ((bf16[16,1,256,256]{3,2,1,0:T(8,128)(2,1)}), bf16[16,1,256,256]{3,2,1,0:T(8,128)(2,1)}, u32[]{:S(2)}, u32[]{:S(2)}) async-start(bf16[16,1,256,256]{3,2,1,0:T(8,128)(2,1)} %bitcast.99), calls=%async_computation.5 | async-start | bytes 4194304 | tf_op jit(solution)/shard_map/all_to_all | solution.py:58
  348.0 2.5 copy-start.2
  367.2 2.4 copy-start.3
Sparse Core Ops, SparseCore 0:
  11.3 62.5 all-gather.1
